TPU v7x, 32 devices: a whole 2x2x4 slice. The times are simulated.
32 devices in a mesh: row: 4 (over z), col: 2 (over y), layer: 4 (over x, core).
Axes of the slice: x: 2, y: 2, z: 4, core: 2. Of those that a mesh axis runs over, the one named last changes fastest.
Arguments:
- amplitudes: float32 [2016, 73536], P('row', ('layer', 'col')), may hold values from -6 to 6
- integrals: float32 [73536, 768], P(('layer', 'col'), 'row'), may hold values from -0.03125 to 0.03125
- occ_energy: float32 [64], replicated, may hold values from -2 to -0.5
- vir_energy: float32 [384], replicated, may hold values from 0.2 to 3
Outputs:
- ladder: float32 [2016, 768], P('col', ('row', 'layer'))
- amplitude_step: float32 [2016, 768], P('col', ('row', 'layer'))
All inputs are finite; a program needn't handle non-finite values.
Results may differ from a plain program's by a relative error of at most 0.00007.
Values sent between devices are 32-bit elements; how exact they have to be, the bound alone decides.
No kernel may reach another device: no remote copies, remote signals or barrier semaphores. Data moves between devices by JAX's collectives and lax.ppermute only.
A program may use at most 128 MiB of HBM per device.

v0:
```python
import jax
import jax.numpy as jnp
import numpy as np
from jax import lax
from jax.sharding import PartitionSpec as P


def lookup(indices, values_table):
    positions = jnp.arange(values_table.shape[0], dtype=jnp.int32)
    picked = jnp.where(indices[:, None] == positions[None, :], values_table[None, :], 0.0)
    return jnp.sum(picked, axis=1)


def owner_blocks(partial_sum):
    col_count = lax.axis_size("col")
    layer_count = lax.axis_size("layer")
    pair_rows = partial_sum.shape[0] // col_count
    slab_cols = partial_sum.shape[1] // layer_count
    blocks = partial_sum.reshape(col_count, pair_rows, layer_count, slab_cols)
    return blocks.transpose(0, 2, 1, 3).reshape(col_count * layer_count * pair_rows, slab_cols)


def shards(amplitudes, integrals, occ_energy, vir_energy):
    partial_rows = jnp.dot(
        amplitudes,
        lax.all_gather(integrals, "row", axis=1, tiled=True),
        precision=lax.Precision.HIGHEST,
        preferred_element_type=jnp.float32,
    )
    partial_sum = lax.all_to_all(partial_rows, "row", split_axis=1, concat_axis=0, tiled=True)
    ladder = lax.psum_scatter(
        owner_blocks(partial_sum), ("col", "layer"), scatter_dimension=0, tiled=True
    )
    pair_rows = ladder.shape[0]
    slab_cols = ladder.shape[1]
    occupied = occ_energy.shape[0]
    virtuals = vir_energy.shape[0]
    first_np, second_np = np.triu_indices(occupied, 1)
    ij_start = lax.axis_index("col") * pair_rows
    ab_start = (
        lax.axis_index("row") * lax.axis_size("layer") + lax.axis_index("layer")
    ) * slab_cols
    first_index = lax.dynamic_slice_in_dim(
        jnp.asarray(first_np, dtype=jnp.int32), ij_start, pair_rows
    )
    second_index = lax.dynamic_slice_in_dim(
        jnp.asarray(second_np, dtype=jnp.int32), ij_start, pair_rows
    )
    pair_sum = lookup(first_index, occ_energy) + lookup(second_index, occ_energy)
    ab_index = ab_start + jnp.arange(slab_cols, dtype=jnp.int32)
    vir_sum = lookup(ab_index // virtuals, vir_energy) + lookup(ab_index % virtuals, vir_energy)
    denominator = pair_sum[:, None] - vir_sum[None, :]
    return (ladder, ladder / denominator)


def solution(mesh):
    in_specs = (P("row", ("layer", "col")), P(("layer", "col"), "row"), P(), P())
    out_specs = (P("col", ("row", "layer")), P("col", ("row", "layer")))
    return jax.shard_map(shards, mesh=mesh, in_specs=in_specs, out_specs=out_specs, check_vma=False)
```

profile of v0, /device:TPU:0, one launch (start us, length us, event | category | flops | bytes accessed | tf_op | source)
XLA Modules:
  0.0 642.0 jit_solution(13388910612487923109)
XLA Ops:
  7.2 0.0 all-gather.2.cloned.1.call-start
  7.2 0.7 all-gather.2.cloned.1.call-update
  7.9 0.0 reduce-scatter.4.cloned.1.call-start
  7.9 480.5 %all-gather.2.cloned.1.call-done = f32[9192,768]{0,1:T(8,128)} async-done(((f32[9192,192]{0,1:T(8,128)}), f32[9192,768]{0,1:T(8,128)}) %all-gather.2.cloned.1.call-update) | async-done | bytes 28237840 | tf_op jit(solution)/shard_map/all_gather | solution.py:26
  488.4 48.5 %fusion.1 = f32[504,768]{0,1:T(8,128)S(1)} fusion(f32[504,9192]{1,0:T(8,128)} %param.6, f32[9192,768]{0,1:T(8,128)} %all-gather.2.cloned.1.call-done), kind=kOutput, calls=%fused_computation.13 | convolution fusion | flops 42695589888 | bytes 48317184 | tf_op jit(solution)/shard_map/dot_general | solution.py:24
  536.9 0.0 copy-start.2
  537.0 0.0 copy-start.1
  537.0 0.0 copy-start.3
  537.0 0.0 copy-start.4
  537.0 40.0 %all_to_all.16 = f32[504,4,192]{0,2,1:T(8,128)S(1)} all-to-all(f32[504,4,192]{0,2,1:T(8,128)S(1)} %bitcast.12), channel_id=1, replica_groups=mesh['row'=4,'col'=2,'layer'=4] {'row'}, dimensions={1} | all-to-all | bytes 3096576 | tf_op jit(solution)/shard_map/all_to_all | solution.py:30
  577.0 1.0 copy.17
  578.0 1.9 reshape.46
  579.9 3.1 copy.22
  583.0 0.0 reduce-scatter.4.cloned.1.call-update
  583.0 0.0 copy-done.2
  583.0 0.1 dynamic_slice.7
  583.1 0.1 dynamic_slice.6
  583.2 0.2 select_reduce_fusion.2
  583.4 0.2 select_reduce_fusion
  583.6 49.5 %reduce-scatter.4.cloned.1.call-done = f32[1008,48]{1,0:T(8,128)} async-done(((f32[8064,48]{1,0:T(8,128)}), f32[1008,48]{1,0:T(8,128)}) %reduce-scatter.4.cloned.1.call-update) | async-done | bytes 193552
  633.1 1.2 copy.21
  634.4 0.0 copy-start
  634.4 0.8 subtract_divide_fusion
  635.1 0.0 copy-done
  (6 shorter events, 0.0 us)
Async XLA Ops:
  7.2 481.3 %all-gather.2.cloned.1.call-start = ((), (), s32[]{:S(2)}) async-start(), calls=%async_computation.2 | async-start | bytes 35389440 | tf_op jit(solution)/shard_map/all_gather | solution.py:26
  7.9 625.2 %reduce-scatter.4.cloned.1.call-start = ((), (), s32[]{:S(2)}) async-start(), calls=%async_computation.3 | async-start | bytes 4644864
  536.9 46.1 %copy-start.2 = (s32[2016]{0:T(1024)S(1)}, s32[2016]{0:T(1024)}, u32[]{:S(2)}) copy-start(s32[2016]{0:T(1024)} %constant.48.clone) | copy-start | bytes 24196
  537.0 46.2 %copy-start.1 = (s32[2016]{0:T(1024)S(1)}, s32[2016]{0:T(1024)}, u32[]{:S(2)}) copy-start(s32[2016]{0:T(1024)} %constant.47.clone) | copy-start | bytes 24196
  537.0 46.2 %copy-start.3 = (f32[384]{0:T(512)S(1)}, f32[384]{0:T(512)}, u32[]{:S(2)}) copy-start(f32[384]{0:T(512)} %param.9) | copy-start | bytes 4612
  537.0 46.4 %copy-start.4 = (f32[64]{0:T(128)S(1)}, f32[64]{0:T(128)}, u32[]{:S(2)}) copy-start(f32[64]{0:T(128)} %param.8) | copy-start | bytes 772
  634.4 0.8 copy-start
Sparse Core Ops, SparseCore 0:
  9.6 478.8 all-gather.1
  583.1 49.9 reduce-scatter.3
where the time goes:
time: 642 us
  waiting for transfers between devices  531 us (83%)
  matrix products  48.5 us (8%)
  blocking collectives  40 us (6%)
  between operations  14.2 us (2%)
  local copies, waits for them, and re-layouts  7.39 us (1%)
    all_gather x1, waiting for transfers between devices, shards(): lax.all_gather(integrals, 'row', axis=1, tiled=True)  480 us
    unnamed x3, waiting for transfers between devices  50.2 us
    dot_general x1, matrix products, shards(): jnp.dot(amplitudes, lax.all_gather(integrals, 'row', axis=1, tiled=True),...  48.5 us
    all_to_all x1, blocking collectives, shards(): lax.all_to_all(partial_rows, 'row', split_axis=1, concat_axis=0, tiled=True)  40 us
  transfers between devices with their start and end apart: 2, of which 2 were waited for; matrix products, arithmetic and copies ran while one was open for 0% of the time, Pallas kernels for 0%

commit v1 on v0

v1 whole, which is shorter than its diff:
```python
import functools

import jax
import jax.numpy as jnp
import numpy as np
from jax import lax
from jax.experimental import pallas as pl
from jax.experimental.pallas import tpu as pltpu
from jax.sharding import PartitionSpec as P


ROW, COL, LAYER = "row", "col", "layer"


def lookup(indices, values_table):
    positions = jnp.arange(values_table.shape[0], dtype=jnp.int32)
    picked = jnp.where(indices[:, None] == positions[None, :], values_table[None, :], 0.0)
    return jnp.sum(picked, axis=1)


def split(values):
    high = values.astype(jnp.bfloat16)
    return high, (values - high.astype(jnp.float32)).astype(jnp.bfloat16)


def product_kernel(depth, step, term_sizes, flag_ref, *refs):
    at = pl.program_id(0)
    term_refs = refs[: sum(term_sizes)]
    source_ref = refs[len(term_refs)]
    start_refs = refs[len(term_refs) + 1 : -1]
    total_ref = refs[-1]

    def valid(values):
        if depth % step == 0:
            return values
        place = lax.broadcasted_iota(jnp.int32, values.shape, 1)
        return jnp.where(place < depth - at * step, values, 0.0)

    blocks = []
    used = 0
    for size in term_sizes:
        block = term_refs[used][...]
        if size == 2:
            other = term_refs[used + 1][...]
            block = jnp.where(flag_ref[0] == 2, block + other, jnp.where(flag_ref[0] == 1, other, block))
        blocks.append(split(valid(block)))
        used += size
    high, low = split(valid(source_ref[...]))

    def dot(a, b):
        return lax.dot_general(a, b, (((1,), (1,)), ((), ())), preferred_element_type=jnp.float32)

    left_high = jnp.concatenate([block for block, _ in blocks], axis=0)
    left = jnp.concatenate([left_high] + [block for _, block in blocks], axis=0)
    half = left_high.shape[0]
    both = dot(left, high)
    part = both[:half] + (both[half:] + dot(left_high, low))

    @pl.when(at == 0)
    def _():
        total_ref[...] = part if not start_refs else start_refs[0][...] + part

    @pl.when(at > 0)
    def _():
        total_ref[...] += part


def products(terms, source, offset, start=None, flag=None):
    chunks = [chunk for term in terms for chunk in term]
    depth, columns = chunks[0].shape
    height = source.shape[0]
    step = next(n for n in (512, 256, 128) if offset % n == 0)
    if depth % step and depth % 256 == 0:
        step = 256
    in_specs = [pl.BlockSpec((columns, step), lambda i, _: (0, i))] * len(chunks)
    in_specs.append(pl.BlockSpec((height, step), lambda i, _: (0, offset // step + i)))
    shape = (len(terms) * columns, height)
    whole = pl.BlockSpec(shape, lambda i, _: (0, 0))
    operands = [chunk.T for chunk in chunks] + [source]
    aliases = {}
    if start is not None:
        aliases = {1 + len(operands): 0}
        in_specs.append(whole)
        operands.append(start)
    flags = jnp.full((1,), 2, jnp.int32) if flag is None else flag.reshape(1).astype(jnp.int32)
    return pl.pallas_call(
        functools.partial(product_kernel, depth, step, tuple(len(t) for t in terms)),
        grid_spec=pltpu.PrefetchScalarGridSpec(
            num_scalar_prefetch=1,
            grid=(pl.cdiv(depth, step),),
            in_specs=in_specs,
            out_specs=whole,
        ),
        out_shape=jax.ShapeDtypeStruct(shape, jnp.float32),
        input_output_aliases=aliases,
        compiler_params=pltpu.CompilerParams(dimension_semantics=("arbitrary",)),
        cost_estimate=pl.CostEstimate(
            flops=2 * depth * shape[0] * height,
            bytes_accessed=4 * depth * (columns * len(chunks) + height),
            transcendentals=0,
        ),
    )(flags, *operands)


def product(chunk, source):
    return lax.dot_general(
        chunk,
        source,
        (((0,), (1,)), ((), ())),
        precision=lax.Precision.HIGH,
        preferred_element_type=jnp.float32,
    )


def total(parts):
    return sum(parts[1:], parts[0])


CHUNKS = 4
KEPT = 2


def chunk_bounds(depth):
    tile = 256
    ends = [depth * share // 1024 // tile * tile for share in (314, 656, 913)]
    return [0] + ends + [depth]


def streamed_blocks(amplitudes, integrals):
    rows = lax.axis_size(ROW)
    plane = lax.axis_index(ROW)
    bounds = chunk_bounds(integrals.shape[0])
    own = [integrals[a:b] for a, b in zip(bounds[:-1], bounds[1:])]

    def hop(values, distance, c):
        low, high = (0, rows - 1) if c < KEPT else (1, rows - 2)
        up = [(p - 1, p) for p in range(distance, rows) if low <= p <= high]
        down = [(rows - 1 - p, rows - 1 - t) for p, t in up]
        upward = lax.ppermute(values[0], ROW, up)
        downward = lax.ppermute(values[1], ROW, down)
        return upward, downward

    near, lent = [], {}
    for c in range(CHUNKS):
        near.append(hop((own[c], own[c]), 1, c))
    for c in range(KEPT, CHUNKS):
        sent = amplitudes[:, bounds[c] : bounds[c + 1]]
        lent[c] = lax.ppermute(sent, ROW, [(0, 1), (rows - 1, rows - 2)])
    middle = [hop(near[c], 2, c) for c in range(CHUNKS)]
    far = [hop(middle[c], 3, c) for c in range(KEPT)]

    lower = (plane < rows // 2).astype(jnp.int32)
    at_end = (plane == 0) | (plane == rows - 1)
    slab = integrals.shape[1]
    self_block = products([(integrals,)], amplitudes, 0)
    nearby, second, lent_inner = None, None, None
    for c in range(CHUNKS):
        nearby = products([(near[c][0],), (near[c][1],)], amplitudes, bounds[c], nearby)
    for c in range(KEPT - 1):
        second = products([middle[c]], amplitudes, bounds[c], second)
    a, b = bounds[KEPT - 1 : KEPT + 1]
    second = second + product(total(middle[KEPT - 1]), amplitudes[:, a:b])
    second = lax.optimization_barrier(second)
    end = CHUNKS - 1
    for c in range(KEPT, end):
        lent_inner = products([(own[c],), near[c]], lent[c], 0, lent_inner, lower)
    late = jnp.where(at_end, 0.0, second)
    second = jnp.where(at_end, second, 0.0)
    for c in range(KEPT - 1):
        late = late + product(total(far[c]), amplitudes[:, bounds[c] : bounds[c + 1]])
    late = lax.optimization_barrier(late)
    lent_late = 0.0
    for c in range(KEPT, end):
        chunk = total(middle[c])
        late = late + product(chunk, amplitudes[:, bounds[c] : bounds[c + 1]])
        lent_late = lent_late + product(chunk, lent[c])
        late, lent_late = lax.optimization_barrier((late, lent_late))
    chosen = jnp.where(plane < rows // 2, near[end][1], near[end][0])
    lent_self = lent_inner[:slab] + product(own[end], lent[end])
    lent_near = lent_inner[slab:] + product(chosen, lent[end])
    late = late + product(total(far[KEPT - 1]), amplitudes[:, a:b])
    chunk = total(middle[end])
    late = late + product(chunk, amplitudes[:, bounds[end] :])
    lent_late = lent_late + product(chunk, lent[end])
    return (self_block, nearby[slab:], nearby[:slab]), (late, lent_late, second + lent_self, lent_near)


def plane_sums(blocks):
    layers, cols = lax.axis_size(LAYER), lax.axis_size(COL)
    layer, col = lax.axis_index(LAYER), lax.axis_index(COL)
    share = blocks[0].shape[0] // (layers * cols)
    pairs = layers // 2
    stacked = jnp.stack(blocks).reshape(len(blocks), pairs, 2, cols, share, -1)

    def pick(values, place, axis):
        return lax.dynamic_index_in_dim(values, place, axis, keepdims=False)

    core = layer % 2
    other = lax.ppermute(pick(stacked, 1 - core, 2), LAYER, [(n, n ^ 1) for n in range(layers)])
    halves = pick(stacked, core, 2) + other
    pair = layer // 2

    def piece(pair_at, col_at):
        return pick(pick(halves, pair_at, 1), col_at, 1)

    sums = piece(pair, col)
    for pair_step in range(pairs):
        for col_step in range(cols):
            if pair_step or col_step:
                moves = [
                    (
                        c * layers + n,
                        (c + col_step) % cols * layers + ((n // 2 + pair_step) % pairs) * 2 + n % 2,
                    )
                    for c in range(cols)
                    for n in range(layers)
                ]
                sent = piece((pair + pair_step) % pairs, (col + col_step) % cols)
                sums = sums + lax.ppermute(sent, (COL, LAYER), moves)
    return sums


def to_owner_col(values):
    rows, cols = lax.axis_size(ROW), lax.axis_size(COL)
    col, plane = lax.axis_index(COL), lax.axis_index(ROW)
    owners = [p * cols // rows for p in range(rows)]
    pairs = [(p * cols + (owners[p] + 1) % cols, p * cols + owners[p]) for p in range(rows)]
    other = lax.ppermute(values, (ROW, COL), pairs)
    first = col == 0
    both = jnp.stack([jnp.where(first, values, other), jnp.where(first, other, values)])
    return jnp.where(col == plane * cols // rows, both, 0.0)


def between_planes(values, moves):
    rows, cols = lax.axis_size(ROW), lax.axis_size(COL)
    pairs = [(s * cols + s * cols // rows, t * cols + s * cols // rows) for s, t in moves]
    return lax.ppermute(values, (ROW, COL), pairs)


def to_owner(values, moves):
    rows, cols = lax.axis_size(ROW), lax.axis_size(COL)
    arrived = []
    for step in range(cols):
        owners = [(s, t, s * cols // rows) for s, t in moves]
        pairs = [(s * cols + (owner + step) % cols, t * cols + owner) for s, t, owner in owners]
        arrived.append(lax.ppermute(values, (ROW, COL), pairs))
    first = lax.axis_index(COL) == 0
    return jnp.stack([jnp.where(first, arrived[0], arrived[1]), jnp.where(first, arrived[1], arrived[0])])


def ladder_by_plane_sums(amplitudes, integrals):
    plane = lax.axis_index(ROW)
    end = lax.axis_size(ROW) - 1
    early, late = streamed_blocks(amplitudes, integrals)
    held = to_owner_col(plane_sums(early))
    above = between_planes(held[:, 1], [(p, p + 1) for p in range(end)])
    below = between_planes(held[:, 2], [(p + 1, p) for p in range(end)])
    inner = (plane > 0) & (plane < end)
    last, lent_last, second, lent_near = plane_sums(late)
    lent_self = to_owner_col(second)
    three = to_owner(jnp.where(inner, lent_near, last), [(0, end), (1, 2), (2, 1), (end, 0)])
    two = jnp.where(inner, jnp.stack([last, lent_last]), jnp.stack([second, jnp.zeros_like(second)]))
    two = to_owner(two, [(0, 2), (1, end), (2, 0), (end, 1)])
    even = held[:, 0] + two[:, 0] + jnp.where(inner, three, 0.0)
    odd = above + below + two[:, 1] + jnp.where(inner, lent_self, three)
    own_first = plane % 2 == 0
    owned = jnp.stack([jnp.where(own_first, even, odd), jnp.where(own_first, odd, even)])
    group, cols, share, height = owned.shape
    return owned.transpose(0, 3, 1, 2).reshape(group * height, cols * share)


def ladder_by_scatter(amplitudes, integrals):
    partial_rows = jnp.dot(
        amplitudes,
        lax.all_gather(integrals, ROW, axis=1, tiled=True),
        precision=lax.Precision.HIGHEST,
        preferred_element_type=jnp.float32,
    )
    partial_sum = lax.all_to_all(partial_rows, ROW, split_axis=1, concat_axis=0, tiled=True)
    col_count = lax.axis_size(COL)
    layer_count = lax.axis_size(LAYER)
    pair_rows = partial_sum.shape[0] // col_count
    slab_cols = partial_sum.shape[1] // layer_count
    blocks = partial_sum.reshape(col_count, pair_rows, layer_count, slab_cols)
    blocks = blocks.transpose(0, 2, 1, 3).reshape(col_count * layer_count * pair_rows, slab_cols)
    return lax.psum_scatter(blocks, (COL, LAYER), scatter_dimension=0, tiled=True)


def denominators(occ_energy, vir_energy, pair_rows, slab_cols):
    occupied = occ_energy.shape[0]
    virtuals = vir_energy.shape[0]
    first_np, second_np = np.triu_indices(occupied, 1)
    ij_start = lax.axis_index(COL) * pair_rows
    ab_start = (
        lax.axis_index(ROW) * lax.axis_size(LAYER) + lax.axis_index(LAYER)
    ) * slab_cols
    first_index = lax.dynamic_slice_in_dim(
        jnp.asarray(first_np, dtype=jnp.int32), ij_start, pair_rows
    )
    second_index = lax.dynamic_slice_in_dim(
        jnp.asarray(second_np, dtype=jnp.int32), ij_start, pair_rows
    )
    pair_sum = lookup(first_index, occ_energy) + lookup(second_index, occ_energy)
    ab_index = ab_start + jnp.arange(slab_cols, dtype=jnp.int32)
    vir_sum = lookup(ab_index // virtuals, vir_energy) + lookup(ab_index % virtuals, vir_energy)
    return pair_sum[:, None] - vir_sum[None, :]


def sums_fit(size_of):
    return size_of(ROW) == 4 and size_of(COL) == 2 and size_of(LAYER) % 2 == 0


def shards(amplitudes, integrals, occ_energy, vir_energy):
    if sums_fit(lax.axis_size):
        ladder = ladder_by_plane_sums(amplitudes, integrals)
    else:
        ladder = ladder_by_scatter(amplitudes, integrals)
    denominator = denominators(occ_energy, vir_energy, ladder.shape[0], ladder.shape[1])
    return (ladder, ladder / denominator)


def solution(mesh):
    in_specs = (P(ROW, (LAYER, COL)), P((LAYER, COL), ROW), P(), P())
    out_specs = (P(COL, (ROW, LAYER)), P(COL, (ROW, LAYER)))
    step = jax.shard_map(shards, mesh=mesh, in_specs=in_specs, out_specs=out_specs, check_vma=False)
    if not sums_fit(mesh.shape.__getitem__):
        return step
    return step
```

time: 642 us -> 544 us (0.85)
  waiting for transfers between devices: 531 us -> 233 us
  starting transfers between devices: 0.08 us -> 156 us
  Pallas kernels: 0 us -> 79.7 us
  blocking collectives: 40 us -> 0 us
  local copies, waits for them, and re-layouts: 7.39 us -> 23 us
  between operations: 14.2 us -> 1.55 us
  matrix products: 48.5 us -> 41.3 us
    all_gather x1 -> x0, waiting for transfers between devices: 480 us -> none  [shards(): lax.all_gather(integrals, 'row', axis=1, tiled=True)]
    ppermute x0 -> x38, waiting for transfers between devices: none -> 233 us  [the longest x10 166 us: hop(): downward = lax.ppermute(values[1], ROW, down)]
    ppermute x0 -> x38, starting transfers between devices: none -> 156 us  [the longest x2 92.4 us: streamed_blocks(): lent[c] = lax.ppermute(sent, ROW, [(0, 1), (rows - 1, rows - 2)])]
    pallas_call x0 -> x7, Pallas kernels: none -> 79.7 us  [products(): pl.pallas_call(functools.partial(product_kernel, depth, step, tuple((len(...]
    unnamed x3 -> x0, waiting for transfers between devices: 50.2 us -> none
    all_to_all x1 -> x0, blocking collectives: 40 us -> none  [shards(): lax.all_to_all(partial_rows, 'row', split_axis=1, concat_axis=0, tiled=True)]
    slice x0 -> x6, local copies, waits for them, and re-layouts: none -> 17.1 us  [the longest x4 11.1 us: streamed_blocks(): own = [integrals[a:b] for a, b in zip(bounds[:-1], bounds[1:])]]
    dot_general x1 -> x9, matrix products: 48.5 us -> 41.3 us  [product(): lax.dot_general(chunk, source, (((0,), (1,)), ((), ())), precision=lax.Pr...]
  transfers between devices with their start and end apart: 2 -> 38, of which waited for: 2 -> 10; matrix products, arithmetic and copies ran while one was open for 0% -> 11% of each run, Pallas kernels for 0% -> 15%
where the time goes in v1:
time: 544 us; the launch traced here: 538 us
  waiting for transfers between devices  233 us (43%)
  starting transfers between devices  156 us (29%)
  Pallas kernels  79.7 us (15%)
  matrix products  41.3 us (8%)
  local copies, waits for them, and re-layouts  23 us (4%)
    ppermute x10, waiting for transfers between devices, hop(): downward = lax.ppermute(values[1], ROW, down)  166 us
    ppermute x2, starting transfers between devices, streamed_blocks(): lent[c] = lax.ppermute(sent, ROW, [(0, 1), (rows - 1, rows - 2)])  92.4 us
    pallas_call x7, Pallas kernels, products(): pl.pallas_call(functools.partial(product_kernel, depth, step, tuple((len(...  79.7 us
    ppermute x10, waiting for transfers between devices, hop(): upward = lax.ppermute(values[0], ROW, up)  48.6 us
    dot_general x9, matrix products, product(): lax.dot_general(chunk, source, (((0,), (1,)), ((), ())), precision=lax.Pr...  41.3 us
    ppermute x10, starting transfers between devices, hop(): upward = lax.ppermute(values[0], ROW, up)  30.7 us
    ppermute x10, starting transfers between devices, hop(): downward = lax.ppermute(values[1], ROW, down)  14.7 us
    ppermute x2, waiting for transfers between devices, to_owner_col(): other = lax.ppermute(values, (ROW, COL), pairs)  11.2 us
  transfers between devices with their start and end apart: 38, of which 10 were waited for; matrix products, arithmetic and copies ran while one was open for 11% of the time, Pallas kernels for 15%

profile of v1, /device:TPU:0, one launch (start us, length us, event | category | flops | bytes accessed | tf_op | source)
XLA Modules:
  0.0 538.3 jit_solution(5183166391351634496)
XLA Ops:
  4.2 6.2 %collective-permute-start.2 = (f32[2304,192]{0,1:T(8,128)}, f32[2304,192]{0,1:T(8,128)}, u32[]{:S(2)}, u32[]{:S(2)}) collective-permute-start(f32[2304,192]{0,1:T(8,128)} %get-tuple-element.13), channel_id=1, source_target_pairs={{0,8},{8,16},{1,9},{9,17},{2,10},{10,18},{3,11},{11,19},{4,12},{12... | collective-permute-start | bytes 5308424 | tf_op jit(solution)/shard_map/ppermute | solution.py:139
  15.5 48.6 %collective-permute-done = f32[1000,192]{0,1:T(8,128)S(1)} collective-permute-done((f32[1000,192]{0,1:T(8,128)S(1)}, f32[1000,192]{0,1:T(8,128)S(1)}, u32[]{:S(2)}, u32[]{:S(2)}) %collective-permute-start) | collective-permute-done | bytes 768032 | tf_op jit(solution)/shard_map/ppermute | solution.py:139
  68.1 8.6 %collective-permute-start.4 = (f32[3072,192]{0,1:T(8,128)}, f32[3072,192]{0,1:T(8,128)}, u32[]{:S(2)}, u32[]{:S(2)}) collective-permute-start(f32[3072,192]{0,1:T(8,128)} %slice.57), channel_id=1, source_target_pairs={{0,8},{8,16},{16,24},{1,9},{9,17},{17,25},{2,10},{10,18},{18,26},{... | collective-permute-start | bytes 7077896 | tf_op jit(solution)/shard_map/ppermute | solution.py:139
  89.8 86.9 %collective-permute-start.26 = (f32[504,1000]{0,1:T(8,128)}, f32[504,1000]{0,1:T(8,128)S(1)}, u32[]{:S(2)}, u32[]{:S(2)}) collective-permute-start(f32[504,1000]{0,1:T(8,128)} %copy.22), channel_id=1, source_target_pairs={{0,8},{24,16},{1,9},{25,17},{2,10},{26,18},{3,11},{27,19},{4,12},{... | collective-permute-start | bytes 6048008 | tf_op jit(solution)/shard_map/ppermute | solution.py:148
  176.7 4.8 slice.64
  181.5 5.5 %collective-permute-start.21 = (f32[504,2304]{1,0:T(8,128)}, f32[504,2304]{1,0:T(8,128)}, u32[]{:S(2)}, u32[]{:S(2)}) collective-permute-start(f32[504,2304]{1,0:T(8,128)} %slice.64), channel_id=1, source_target_pairs={{0,8},{24,16},{1,9},{25,17},{2,10},{26,18},{3,11},{27,19},{4,12},{... | collective-permute-start | bytes 13934600 | tf_op jit(solution)/shard_map/ppermute | solution.py:148
  190.8 19.5 %shard_map.77 = f32[192,504]{1,0:T(8,128)} custom-call(s32[1]{0:T(128)} %constant.362.clone.1.flag_ref, f32[192,9192]{1,0:T(8,128)} %bitcast.114, f32[504,9192]{1,0:T(8,128)} %refs_2_.9), custom_call_target="tpu_custom_call" | custom-call | flops 1778982912 | bytes 25590528 | tf_op jit(solution)/shard_map/pallas_call | solution.py:86
  211.8 11.8 %shard_map.78.refs_3_ = f32[384,504]{1,0:T(8,128)} custom-call(s32[1]{0:T(128)} %constant.362.clone.1.flag_ref, f32[192,2816]{1,0:T(8,128)} %bitcast.8.refs_0_, f32[192,2816]{1,0:T(8,128)} %bitcast.9.refs_1_, f32[504,9192]{1,0:T(8,128)} %refs_2_.9), custom_call_target="tpu_custom_call" | custom-call | flops 1089994752 | bytes 10002432 | tf_op jit(solution)/shard_map/pallas_call | solution.py:86
  223.6 12.8 %shard_map.79.refs_3_ = f32[384,504]{1,0:T(8,128)} custom-call(s32[1]{0:T(128)} %constant.362.clone.1.flag_ref, f32[192,3072]{1,0:T(8,128)} %bitcast.6.refs_0_, f32[192,3072]{1,0:T(8,128)} %bitcast.7.refs_1_, f32[504,9192]{1,0:T(8,128)} %refs_2_.9, f32[384,504]{1,0:T(8,128)} %shard_map.78.refs_3_), custom_call_target="tpu_custom_call", output_to_operand_aliasing={{}: (4, {})} | custom-call | flops 1189085184 | bytes 10911744 | tf_op jit(solution)/shard_map/pallas_call | solution.py:86
  236.4 10.3 %shard_map.80.refs_3_ = f32[384,504]{1,0:T(8,128)} custom-call(s32[1]{0:T(128)} %constant.362.clone.1.flag_ref, f32[192,2304]{1,0:T(8,128)} %bitcast.4.refs_0_.refs_1_, f32[192,2304]{1,0:T(8,128)} %bitcast.5.refs_1_.refs_2_, f32[504,9192]{1,0:T(8,128)} %refs_2_.9, f32[384,504]{1,0:T(8,128)} %shard_map.79.refs_3_), custom_call_target="tpu_custom_call", output_to_operand_aliasing={{}: (4, {})} | custom-call | flops 891813888 | bytes 8183808 | tf_op jit(solution)/shard_map/pallas_call | solution.py:86
  246.7 4.5 shard_map.81
  261.7 4.0 fusion.36
  272.2 124.3 %collective-permute-done.14 = f32[2816,192]{0,1:T(8,128)} collective-permute-done((f32[2816,192]{0,1:T(8,128)}, f32[2816,192]{0,1:T(8,128)}, u32[]{:S(2)}, u32[]{:S(2)}) %collective-permute-start.14) | collective-permute-done | bytes 2162720 | tf_op jit(solution)/shard_map/ppermute | solution.py:140
  401.3 5.5 %fusion.28 = f32[192,504]{1,0:T(8,128)S(1)} fusion(f32[2304,192]{0,1:T(8,128)} %collective-permute-done.19, f32[2304,192]{0,1:T(8,128)} %collective-permute-done.20, f32[504,9192]{1,0:T(8,128)} %refs_2_.9), kind=kOutput, calls=%fused_computation.20 | convolution fusion | flops 1338163200 | bytes 8570880 | tf_op jit(solution)/shard_map/dot_general | solution.py:106
  406.8 10.5 %shard_map.82 = f32[192,504]{1,0:T(8,128)} custom-call(s32[1]{0:T(128)} %constant.362.clone.1.flag_ref, f32[192,2816]{1,0:T(8,128)} %bitcast.21.refs_0_, f32[192,2816]{1,0:T(8,128)} %bitcast.22.refs_1_, f32[504,9192]{1,0:T(8,128)} %refs_2_.9), custom_call_target="tpu_custom_call" | custom-call | flops 544997376 | bytes 10002432 | tf_op jit(solution)/shard_map/pallas_call | solution.py:86
  418.8 10.4 %shard_map.83 = f32[384,504]{1,0:T(8,128)} custom-call(s32[1]{0:T(128)} %bitcast.25.flag_ref, f32[192,2304]{1,0:T(8,128)} %get-tuple-element.14.refs_0_, f32[192,2304]{1,0:T(8,128)} %bitcast.4.refs_0_.refs_1_, f32[192,2304]{1,0:T(8,128)} %bitcast.5.refs_1_.refs_2_, f32[504,2304]{1,0:T(8,128)} %collective-permute-done.21.refs_3_), custom_call_target="tpu_custom_call" | custom-call | flops 891813888 | bytes 9953280 | tf_op jit(solution)/shard_map/pallas_call | solution.py:86
  431.4 5.7 %fusion.26 = f32[192,504]{1,0:T(8,128)S(1)} fusion(f32[504,2304]{1,0:T(8,128)} %collective-permute-done.21.refs_3_, f32[2304,192]{0,1:T(8,128)} %collective-permute-done.19, f32[2304,192]{0,1:T(8,128)} %collective-permute-done.20), kind=kOutput, calls=%fused_computation.18 | convolution fusion | flops 1338163200 | bytes 8570880 | tf_op jit(solution)/shard_map/dot_general | solution.py:106
  437.1 7.1 %fusion.2 = f32[192,504]{1,0:T(8,128)S(1)} fusion(f32[504,9192]{1,0:T(8,128)} %refs_2_.9, f32[3072,192]{0,1:T(8,128)} %collective-permute-done.15, f32[3072,192]{0,1:T(8,128)} %collective-permute-done.16), kind=kOutput, calls=%fused_computation.2 | convolution fusion | flops 1784217600 | bytes 11298816 | tf_op jit(solution)/shard_map/dot_general | solution.py:106
  450.1 6.4 %fusion.9 = f32[192,504]{1,0:T(8,128)S(1)} fusion(f32[504,9192]{1,0:T(8,128)} %refs_2_.9, f32[2816,192]{0,1:T(8,128)} %collective-permute-done.17, f32[2816,192]{0,1:T(8,128)} %collective-permute-done.18, f32[192,504]{1,0:T(8,128)S(1)} %add.281, pred[]{:T(512)S(6)} %or.3), kind=kOutput, calls=%fused_computation.10 | convolution fusion | flops 1635726336 | bytes 10776577 | tf_op jit(solution)/shard_map/dot_general | solution.py:106
  456.7 41.1 %collective-permute-done.23 = f32[3072,192]{0,1:T(8,128)} collective-permute-done((f32[3072,192]{0,1:T(8,128)}, f32[3072,192]{0,1:T(8,128)}, u32[]{:S(2)}, u32[]{:S(2)}) %collective-permute-start.23) | collective-permute-done | bytes 2359328 | tf_op jit(solution)/shard_map/ppermute | solution.py:140
  497.8 5.4 %fusion.19 = f32[192,504]{1,0:T(8,128)S(1)} fusion(f32[192,504]{1,0:T(8,128)S(1)} %copy-done.6, f32[192,504]{1,0:T(8,128)S(1)} %add.285, f32[504,9192]{1,0:T(8,128)S(1)} %bitcast.113, f32[3072,192]{0,1:T(8,128)} %collective-permute-done.22, f32[3072,192]{0,1:T(8,128)} %collective-permute-done.23), kind=kOutput, calls=%fused_computation.12 | convolution fusion | flops 1784411136 | bytes 12085248 | tf_op jit(solution)/shard_map/dot_general | solution.py:106
  506.2 6.5 %collective-permute-done.12 = f32[3,24,504]{2,1,0:T(8,128)S(1)} collective-permute-done((f32[3,24,504]{2,1,0:T(8,128)S(1)}, f32[3,24,504]{2,1,0:T(8,128)S(1)}, u32[]{:S(2)}, u32[]{:S(2)}) %collective-permute-start.12) | collective-permute-done | bytes 145184 | tf_op jit(solution)/shard_map/ppermute | solution.py:228
  521.0 4.0 collective-permute-done.30
  528.4 4.7 collective-permute-done.37
  (155 shorter events, 81.9 us)
Async XLA Ops:
  4.2 82.4 %collective-permute-start.2 = (f32[2304,192]{0,1:T(8,128)}, f32[2304,192]{0,1:T(8,128)}, u32[]{:S(2)}, u32[]{:S(2)}) collective-permute-start(f32[2304,192]{0,1:T(8,128)} %get-tuple-element.13), channel_id=1, source_target_pairs={{0,8},{8,16},{1,9},{9,17},{2,10},{10,18},{3,11},{11,19},{4,12},{12... | collective-permute-start | bytes 5308424 | tf_op jit(solution)/shard_map/ppermute | solution.py:139
  11.6 52.5 %collective-permute-start = (f32[1000,192]{0,1:T(8,128)S(1)}, f32[1000,192]{0,1:T(8,128)S(1)}, u32[]{:S(2)}, u32[]{:S(2)}) collective-permute-start(f32[1000,192]{0,1:T(8,128)S(1)} %slice.55), channel_id=1, source_target_pairs={{0,8},{8,16},{1,9},{9,17},{2,10},{10,18},{3,11},{11,19},{4,12},{12... | collective-permute-start | bytes 2304008 | tf_op jit(solution)/shard_map/ppermute | solution.py:139
  13.9 68.7 %collective-permute-start.1 = (f32[1000,192]{0,1:T(8,128)S(1)}, f32[1000,192]{0,1:T(8,128)}, u32[]{:S(2)}, u32[]{:S(2)}) collective-permute-start(f32[1000,192]{0,1:T(8,128)S(1)} %slice.55), channel_id=1, source_target_pairs={{24,16},{16,8},{25,17},{17,9},{26,18},{18,10},{27,19},{19,11},{28,... | collective-permute-start | bytes 2304008 | tf_op jit(solution)/shard_map/ppermute | solution.py:140
  64.1 19.8 %collective-permute-start.24 = (f32[1000,192]{0,1:T(8,128)S(1)}, f32[1000,192]{0,1:T(8,128)S(1)}, u32[]{:S(2)}, u32[]{:S(2)}) collective-permute-start(f32[1000,192]{0,1:T(8,128)S(1)} %collective-permute-done), channel_id=1, source_target_pairs={{8,16},{9,17},{10,18},{11,19},{12,20},{13,21},{14,22},{15,23}} | collective-permute-start | bytes 2304008 | tf_op jit(solution)/shard_map/ppermute | solution.py:139
  68.1 120.9 %collective-permute-start.4 = (f32[3072,192]{0,1:T(8,128)}, f32[3072,192]{0,1:T(8,128)}, u32[]{:S(2)}, u32[]{:S(2)}) collective-permute-start(f32[3072,192]{0,1:T(8,128)} %slice.57), channel_id=1, source_target_pairs={{0,8},{8,16},{16,24},{1,9},{9,17},{17,25},{2,10},{10,18},{18,26},{... | collective-permute-start | bytes 7077896 | tf_op jit(solution)/shard_map/ppermute | solution.py:139
  79.8 101.7 %collective-permute-start.6 = (f32[2816,192]{0,1:T(8,128)}, f32[2816,192]{0,1:T(8,128)}, u32[]{:S(2)}, u32[]{:S(2)}) collective-permute-start(f32[2816,192]{0,1:T(8,128)} %slice.58), channel_id=1, source_target_pairs={{0,8},{8,16},{16,24},{1,9},{9,17},{17,25},{2,10},{10,18},{18,26},{... | collective-permute-start | bytes 6488072 | tf_op jit(solution)/shard_map/ppermute | solution.py:139
  82.6 127.7 %collective-permute-start.5 = (f32[3072,192]{0,1:T(8,128)}, f32[3072,192]{0,1:T(8,128)}, u32[]{:S(2)}, u32[]{:S(2)}) collective-permute-start(f32[3072,192]{0,1:T(8,128)} %slice.57), channel_id=1, source_target_pairs={{24,16},{16,8},{8,0},{25,17},{17,9},{9,1},{26,18},{18,10},{10,2},{... | collective-permute-start | bytes 7077896 | tf_op jit(solution)/shard_map/ppermute | solution.py:140
  86.6 100.4 %collective-permute-start.7 = (f32[2816,192]{0,1:T(8,128)}, f32[2816,192]{0,1:T(8,128)}, u32[]{:S(2)}, u32[]{:S(2)}) collective-permute-start(f32[2816,192]{0,1:T(8,128)} %slice.58), channel_id=1, source_target_pairs={{24,16},{16,8},{8,0},{25,17},{17,9},{9,1},{26,18},{18,10},{10,2},{... | collective-permute-start | bytes 6488072 | tf_op jit(solution)/shard_map/ppermute | solution.py:140
  89.8 163.8 %collective-permute-start.26 = (f32[504,1000]{0,1:T(8,128)}, f32[504,1000]{0,1:T(8,128)S(1)}, u32[]{:S(2)}, u32[]{:S(2)}) collective-permute-start(f32[504,1000]{0,1:T(8,128)} %copy.22), channel_id=1, source_target_pairs={{0,8},{24,16},{1,9},{25,17},{2,10},{26,18},{3,11},{27,19},{4,12},{... | collective-permute-start | bytes 6048008 | tf_op jit(solution)/shard_map/ppermute | solution.py:148
  181.5 235.8 %collective-permute-start.21 = (f32[504,2304]{1,0:T(8,128)}, f32[504,2304]{1,0:T(8,128)}, u32[]{:S(2)}, u32[]{:S(2)}) collective-permute-start(f32[504,2304]{1,0:T(8,128)} %slice.64), channel_id=1, source_target_pairs={{0,8},{24,16},{1,9},{25,17},{2,10},{26,18},{3,11},{27,19},{4,12},{... | collective-permute-start | bytes 13934600 | tf_op jit(solution)/shard_map/ppermute | solution.py:148
  187.0 70.8 %collective-permute-start.19 = (f32[2304,192]{0,1:T(8,128)}, f32[2304,192]{0,1:T(8,128)}, u32[]{:S(2)}, u32[]{:S(2)}) collective-permute-start(f32[2304,192]{0,1:T(8,128)} %collective-permute-done.2), channel_id=1, source_target_pairs={{8,16},{9,17},{10,18},{11,19},{12,20},{13,21},{14,22},{15,23}} | collective-permute-start | bytes 5308424 | tf_op jit(solution)/shard_map/ppermute | solution.py:139
  188.9 71.0 %collective-permute-start.20 = (f32[2304,192]{0,1:T(8,128)}, f32[2304,192]{0,1:T(8,128)}, u32[]{:S(2)}, u32[]{:S(2)}) collective-permute-start(f32[2304,192]{0,1:T(8,128)} %collective-permute-done.3), channel_id=1, source_target_pairs={{16,8},{17,9},{18,10},{19,11},{20,12},{21,13},{22,14},{23,15}} | collective-permute-start | bytes 5308424 | tf_op jit(solution)/shard_map/ppermute | solution.py:140
  210.3 43.3 %collective-permute-start.25 = (f32[1000,192]{0,1:T(8,128)}, f32[1000,192]{0,1:T(8,128)}, u32[]{:S(2)}, u32[]{:S(2)}) collective-permute-start(f32[1000,192]{0,1:T(8,128)} %collective-permute-done.1), channel_id=1, source_target_pairs={{16,8},{17,9},{18,10},{19,11},{20,12},{21,13},{22,14},{23,15}} | collective-permute-start | bytes 2304008 | tf_op jit(solution)/shard_map/ppermute | solution.py:140
  253.7 144.0 %collective-permute-start.15 = (f32[3072,192]{0,1:T(8,128)}, f32[3072,192]{0,1:T(8,128)}, u32[]{:S(2)}, u32[]{:S(2)}) collective-permute-start(f32[3072,192]{0,1:T(8,128)} %collective-permute-done.4), channel_id=1, source_target_pairs={{8,16},{16,24},{9,17},{17,25},{10,18},{18,26},{11,19},{19,27},{12,... | collective-permute-start | bytes 7077896 | tf_op jit(solution)/shard_map/ppermute | solution.py:139
  256.6 143.3 %collective-permute-start.16 = (f32[3072,192]{0,1:T(8,128)}, f32[3072,192]{0,1:T(8,128)}, u32[]{:S(2)}, u32[]{:S(2)}) collective-permute-start(f32[3072,192]{0,1:T(8,128)} %collective-permute-done.5), channel_id=1, source_target_pairs={{16,8},{8,0},{17,9},{9,1},{18,10},{10,2},{19,11},{11,3},{20,12},{1... | collective-permute-start | bytes 7077896 | tf_op jit(solution)/shard_map/ppermute | solution.py:140
  259.9 136.5 %collective-permute-start.14 = (f32[2816,192]{0,1:T(8,128)}, f32[2816,192]{0,1:T(8,128)}, u32[]{:S(2)}, u32[]{:S(2)}) collective-permute-start(f32[2816,192]{0,1:T(8,128)} %collective-permute-done.7), channel_id=1, source_target_pairs={{16,8},{8,0},{17,9},{9,1},{18,10},{10,2},{19,11},{11,3},{20,12},{1... | collective-permute-start | bytes 6488072 | tf_op jit(solution)/shard_map/ppermute | solution.py:140
  270.1 176.3 %collective-permute-start.17 = (f32[2816,192]{0,1:T(8,128)}, f32[2816,192]{0,1:T(8,128)}, u32[]{:S(2)}, u32[]{:S(2)}) collective-permute-start(f32[2816,192]{0,1:T(8,128)} %collective-permute-done.13), channel_id=1, source_target_pairs={{16,24},{17,25},{18,26},{19,27},{20,28},{21,29},{22,30},{23,31}} | collective-permute-start | bytes 6488072 | tf_op jit(solution)/shard_map/ppermute | solution.py:139
  396.4 52.1 %collective-permute-start.18 = (f32[2816,192]{0,1:T(8,128)}, f32[2816,192]{0,1:T(8,128)}, u32[]{:S(2)}, u32[]{:S(2)}) collective-permute-start(f32[2816,192]{0,1:T(8,128)} %collective-permute-done.14), channel_id=1, source_target_pairs={{8,0},{9,1},{10,2},{11,3},{12,4},{13,5},{14,6},{15,7}} | collective-permute-start | bytes 6488072 | tf_op jit(solution)/shard_map/ppermute | solution.py:140
  397.7 58.9 %collective-permute-start.22 = (f32[3072,192]{0,1:T(8,128)}, f32[3072,192]{0,1:T(8,128)}, u32[]{:S(2)}, u32[]{:S(2)}) collective-permute-start(f32[3072,192]{0,1:T(8,128)} %collective-permute-done.15), channel_id=1, source_target_pairs={{16,24},{17,25},{18,26},{19,27},{20,28},{21,29},{22,30},{23,31}} | collective-permute-start | bytes 7077896 | tf_op jit(solution)/shard_map/ppermute | solution.py:139
  399.8 97.9 %collective-permute-start.23 = (f32[3072,192]{0,1:T(8,128)}, f32[3072,192]{0,1:T(8,128)}, u32[]{:S(2)}, u32[]{:S(2)}) collective-permute-start(f32[3072,192]{0,1:T(8,128)} %collective-permute-done.16), channel_id=1, source_target_pairs={{8,0},{9,1},{10,2},{11,3},{12,4},{13,5},{14,6},{15,7}} | collective-permute-start | bytes 7077896 | tf_op jit(solution)/shard_map/ppermute | solution.py:140
  417.3 86.3 %collective-permute-start.10 = (f32[3,24,504]{2,1,0:T(8,128)}, f32[3,24,504]{2,1,0:T(8,128)}, u32[]{:S(2)}, u32[]{:S(2)}) collective-permute-start(f32[3,24,504]{2,1,0:T(8,128)} %get-tuple-element.22), channel_id=1, source_target_pairs={{0,2},{1,3},{2,0},{3,1},{4,6},{5,7},{6,4},{7,5},{8,10},{9,11},{10,... | collective-permute-start | bytes 435464 | tf_op jit(solution)/shard_map/ppermute | solution.py:219
  446.5 57.1 %collective-permute-start.11 = (f32[3,24,504]{2,1,0:T(8,128)S(1)}, f32[3,24,504]{2,1,0:T(8,128)S(1)}, u32[]{:S(2)}, u32[]{:S(2)}) collective-permute-start(f32[3,24,504]{2,1,0:T(8,128)S(1)} %get-tuple-element.21), channel_id=1, source_target_pairs={{0,6},{1,7},{2,4},{3,5},{4,2},{5,3},{6,0},{7,1},{8,14},{9,15},{10,... | collective-permute-start | bytes 435464 | tf_op jit(solution)/shard_map/ppermute | solution.py:219
  448.6 55.1 %collective-permute-start.9 = (f32[3,24,504]{2,1,0:T(8,128)S(1)}, f32[3,24,504]{2,1,0:T(8,128)S(1)}, u32[]{:S(2)}, u32[]{:S(2)}) collective-permute-start(f32[3,24,504]{2,1,0:T(8,128)S(1)} %get-tuple-element.20), channel_id=1, source_target_pairs={{0,4},{1,5},{2,6},{3,7},{4,0},{5,1},{6,2},{7,3},{8,12},{9,13},{10,... | collective-permute-start | bytes 435464 | tf_op jit(solution)/shard_map/ppermute | solution.py:219
  516.7 20.1 %collective-permute-start.35 = (f32[2,24,504]{2,1,0:T(8,128)S(1)}, f32[2,24,504]{2,1,0:T(8,128)S(1)}, u32[]{:S(2)}, u32[]{:S(2)}) collective-permute-start(f32[2,24,504]{2,1,0:T(8,128)S(1)} %get-tuple-element.24), channel_id=1, source_target_pairs={{0,8},{8,16},{20,28},{1,9},{9,17},{21,29},{2,10},{10,18},{22,30},{... | collective-permute-start | bytes 290312 | tf_op jit(solution)/shard_map/ppermute | solution.py:237
  (36 other events, 533.7 us)

commit v2 on v1

--- a/solution.py
+++ b/solution.py
@@ -116,13 +116,14 @@
     return sum(parts[1:], parts[0])
 
 
-CHUNKS = 4
+CHUNKS = 5
 KEPT = 2
+LOANS = ((2, 3), (4,))
 
 
 def chunk_bounds(depth):
     tile = 256
-    ends = [depth * share // 1024 // tile * tile for share in (314, 656, 913)]
+    ends = [depth * share // 1024 // tile * tile for share in (314, 656, 799, 913)]
     return [0] + ends + [depth]
 
 
@@ -143,11 +144,22 @@
     near, lent = [], {}
     for c in range(CHUNKS):
         near.append(hop((own[c], own[c]), 1, c))
-    for c in range(KEPT, CHUNKS):
-        sent = amplitudes[:, bounds[c] : bounds[c + 1]]
-        lent[c] = lax.ppermute(sent, ROW, [(0, 1), (rows - 1, rows - 2)])
+    for group in LOANS:
+        first = bounds[group[0]]
+        sent = amplitudes[:, first : bounds[group[-1] + 1]]
+        loan = lax.ppermute(sent, ROW, [(0, 1), (rows - 1, rows - 2)])
+        for c in group:
+            lent[c] = (loan, bounds[c] - first)
+
+    def lent_part(c):
+        loan, offset = lent[c]
+        return loan[:, offset : offset + bounds[c + 1] - bounds[c]]
+
     middle = [hop(near[c], 2, c) for c in range(CHUNKS)]
-    far = [hop(middle[c], 3, c) for c in range(KEPT)]
+    joined = [lax.optimization_barrier(total(middle[c])) for c in range(KEPT)]
+    far = []
+    for c in range(KEPT):
+        far.append(lax.ppermute(joined[c], ROW, [(1, 0), (rows - 2, rows - 1)]))
 
     lower = (plane < rows // 2).astype(jnp.int32)
     at_end = (plane == 0) | (plane == rows - 1)
@@ -157,31 +169,31 @@
     for c in range(CHUNKS):
         nearby = products([(near[c][0],), (near[c][1],)], amplitudes, bounds[c], nearby)
     for c in range(KEPT - 1):
-        second = products([middle[c]], amplitudes, bounds[c], second)
+        second = products([(joined[c],)], amplitudes, bounds[c], second)
     a, b = bounds[KEPT - 1 : KEPT + 1]
-    second = second + product(total(middle[KEPT - 1]), amplitudes[:, a:b])
+    second = second + product(joined[KEPT - 1], amplitudes[:, a:b])
     second = lax.optimization_barrier(second)
     end = CHUNKS - 1
     for c in range(KEPT, end):
-        lent_inner = products([(own[c],), near[c]], lent[c], 0, lent_inner, lower)
+        lent_inner = products([(own[c],), near[c]], *lent[c], lent_inner, lower)
     late = jnp.where(at_end, 0.0, second)
     second = jnp.where(at_end, second, 0.0)
     for c in range(KEPT - 1):
-        late = late + product(total(far[c]), amplitudes[:, bounds[c] : bounds[c + 1]])
+        late = late + product(far[c], amplitudes[:, bounds[c] : bounds[c + 1]])
     late = lax.optimization_barrier(late)
     lent_late = 0.0
     for c in range(KEPT, end):
         chunk = total(middle[c])
         late = late + product(chunk, amplitudes[:, bounds[c] : bounds[c + 1]])
-        lent_late = lent_late + product(chunk, lent[c])
+        lent_late = lent_late + product(chunk, lent_part(c))
         late, lent_late = lax.optimization_barrier((late, lent_late))
     chosen = jnp.where(plane < rows // 2, near[end][1], near[end][0])
-    lent_self = lent_inner[:slab] + product(own[end], lent[end])
-    lent_near = lent_inner[slab:] + product(chosen, lent[end])
-    late = late + product(total(far[KEPT - 1]), amplitudes[:, a:b])
+    lent_self = lent_inner[:slab] + product(own[end], lent_part(end))
+    lent_near = lent_inner[slab:] + product(chosen, lent_part(end))
+    late = late + product(far[KEPT - 1], amplitudes[:, a:b])
     chunk = total(middle[end])
     late = late + product(chunk, amplitudes[:, bounds[end] :])
-    lent_late = lent_late + product(chunk, lent[end])
+    lent_late = lent_late + product(chunk, lent_part(end))
     return (self_block, nearby[slab:], nearby[:slab]), (late, lent_late, second + lent_self, lent_near)
 
 

time: 544 us -> 528 us (0.971)
  starting transfers between devices: 156 us -> 77.4 us
  waiting for transfers between devices: 233 us -> 294 us
  matrix products: 41.3 us -> 32.6 us
  other arithmetic: 4.37 us -> 12.1 us
    ppermute x10, waiting for transfers between devices: 166 us -> 7.85 us  [hop(): downward = lax.ppermute(values[1], ROW, down)]
    ppermute x10, waiting for transfers between devices: 48.6 us -> 202 us  [hop(): upward = lax.ppermute(values[0], ROW, up)]
    ppermute x2 -> x4, starting transfers between devices: 92.4 us -> 14.7 us  [the longest x2 11.8 us: streamed_blocks(): loan = lax.ppermute(sent, ROW, [(0, 1), (rows - 1, rows - 2)])]
    ppermute x2 -> x4, waiting for transfers between devices: 0.01 us -> 66.2 us  [the longest x2 66.2 us: streamed_blocks(): far.append(lax.ppermute(joined[c], ROW, [(1, 0), (rows - 2, rows - 1)]))]
    dot_general x9 -> x11, matrix products: 41.3 us -> 32.6 us  [product(): lax.dot_general(chunk, source, (((0,), (1,)), ((), ())), precision=lax.Pr...]
    add x2 -> x4, other arithmetic: 0.12 us -> 6.82 us  [the longest x2 6.7 us: total(): return sum(parts[1:], parts[0])]
    pallas_call x7 -> x9, Pallas kernels: 79.7 us -> 82.4 us  [products(): pl.pallas_call(functools.partial(product_kernel, depth, step, tuple((len(...]
    slice x4 -> x5, local copies, waits for them, and re-layouts: 11.1 us -> 10.7 us  [streamed_blocks(): own = [integrals[a:b] for a, b in zip(bounds[:-1], bounds[1:])]]
  transfers between devices with their start and end apart: 38 -> 40, of which waited for: 10 -> 12; matrix products, arithmetic and copies ran while one was open for 11% -> 12% of each run, Pallas kernels for 15% -> 16%
where the time goes in v2:
time: 528 us; the launch traced here: 522 us
  waiting for transfers between devices  294 us (56%)
  Pallas kernels  82.4 us (16%)
  starting transfers between devices  77.4 us (15%)
  matrix products  32.6 us (6%)
  local copies, waits for them, and re-layouts  22.1 us (4%)
  other arithmetic  12.1 us (2%)
    ppermute x10, waiting for transfers between devices, hop(): upward = lax.ppermute(values[0], ROW, up)  202 us
    pallas_call x9, Pallas kernels, products(): pl.pallas_call(functools.partial(product_kernel, depth, step, tuple((len(...  82.4 us
    ppermute x2, waiting for transfers between devices, streamed_blocks(): far.append(lax.ppermute(joined[c], ROW, [(1, 0), (rows - 2, rows - 1)]))  66.2 us
    dot_general x11, matrix products, product(): lax.dot_general(chunk, source, (((0,), (1,)), ((), ())), precision=lax.Pr...  32.6 us
    ppermute x10, starting transfers between devices, hop(): upward = lax.ppermute(values[0], ROW, up)  29.3 us
    ppermute x2, starting transfers between devices, streamed_blocks(): loan = lax.ppermute(sent, ROW, [(0, 1), (rows - 1, rows - 2)])  11.8 us
    ppermute x10, starting transfers between devices, hop(): downward = lax.ppermute(values[1], ROW, down)  11.2 us
    ppermute x2, waiting for transfers between devices, to_owner_col(): other = lax.ppermute(values, (ROW, COL), pairs)  11.2 us
  transfers between devices with their start and end apart: 40, of which 12 were waited for; matrix products, arithmetic and copies ran while one was open for 12% of the time, Pallas kernels for 16%

profile of v2, /device:TPU:0, one launch (start us, length us, event | category | flops | bytes accessed | tf_op | source)
XLA Modules:
  0.0 522.4 jit_solution(15755352691293027513)
XLA Ops:
  1.8 5.0 collective-permute-start
  9.3 5.4 %collective-permute-start.8 = (f32[2816,192]{0,1:T(8,128)S(1)}, f32[2816,192]{0,1:T(8,128)}, u32[]{:S(2)}, u32[]{:S(2)}) collective-permute-start(f32[2816,192]{0,1:T(8,128)S(1)} %slice.73), channel_id=1, source_target_pairs={{0,8},{8,16},{16,24},{1,9},{9,17},{17,25},{2,10},{10,18},{18,26},{... | collective-permute-start | bytes 6488072 | tf_op jit(solution)/shard_map/ppermute | solution.py:140
  27.9 60.0 %collective-permute-done.2 = f32[1024,192]{0,1:T(8,128)S(1)} collective-permute-done((f32[1024,192]{0,1:T(8,128)S(1)}, f32[1024,192]{0,1:T(8,128)S(1)}, u32[]{:S(2)}, u32[]{:S(2)}) %collective-permute-start.2) | collective-permute-done | bytes 786464 | tf_op jit(solution)/shard_map/ppermute | solution.py:140
  89.9 17.9 %collective-permute-done.4 = f32[1280,192]{0,1:T(8,128)} collective-permute-done((f32[1280,192]{0,1:T(8,128)S(1)}, f32[1280,192]{0,1:T(8,128)}, u32[]{:S(2)}, u32[]{:S(2)}) %collective-permute-start.4) | collective-permute-done | bytes 983072 | tf_op jit(solution)/shard_map/ppermute | solution.py:140
  108.6 4.8 slice.80
  113.4 7.3 %collective-permute-start.22 = (f32[504,2304]{1,0:T(8,128)}, f32[504,2304]{1,0:T(8,128)}, u32[]{:S(2)}, u32[]{:S(2)}) collective-permute-start(f32[504,2304]{1,0:T(8,128)} %slice.80), channel_id=1, source_target_pairs={{0,8},{24,16},{1,9},{25,17},{2,10},{26,18},{3,11},{27,19},{4,12},{... | collective-permute-start | bytes 13934600 | tf_op jit(solution)/shard_map/ppermute | solution.py:150
  124.0 5.6 %collective-permute-start.6 = (f32[3072,192]{0,1:T(8,128)}, f32[3072,192]{0,1:T(8,128)}, u32[]{:S(2)}, u32[]{:S(2)}) collective-permute-start(f32[3072,192]{0,1:T(8,128)} %slice.72), channel_id=1, source_target_pairs={{0,8},{8,16},{16,24},{1,9},{9,17},{17,25},{2,10},{10,18},{18,26},{... | collective-permute-start | bytes 7077896 | tf_op jit(solution)/shard_map/ppermute | solution.py:140
  132.9 7.8 %collective-permute-done.9 = f32[2816,192]{0,1:T(8,128)} collective-permute-done((f32[2816,192]{0,1:T(8,128)S(1)}, f32[2816,192]{0,1:T(8,128)}, u32[]{:S(2)}, u32[]{:S(2)}) %collective-permute-start.9) | collective-permute-done | bytes 2162720 | tf_op jit(solution)/shard_map/ppermute | solution.py:141
  143.9 124.0 %collective-permute-done.6 = f32[3072,192]{0,1:T(8,128)} collective-permute-done((f32[3072,192]{0,1:T(8,128)}, f32[3072,192]{0,1:T(8,128)}, u32[]{:S(2)}, u32[]{:S(2)}) %collective-permute-start.6) | collective-permute-done | bytes 2359328 | tf_op jit(solution)/shard_map/ppermute | solution.py:140
  275.8 19.5 %shard_map.77 = f32[192,504]{1,0:T(8,128)} custom-call(s32[1]{0:T(128)} %constant.362.clone.1.flag_ref, f32[192,9192]{1,0:T(8,128)} %bitcast.119, f32[504,9192]{1,0:T(8,128)} %refs_1_.3), custom_call_target="tpu_custom_call" | custom-call | flops 1778982912 | bytes 25590528 | tf_op jit(solution)/shard_map/pallas_call | solution.py:86
  295.3 11.8 %shard_map.78.refs_3_ = f32[384,504]{1,0:T(8,128)} custom-call(s32[1]{0:T(128)} %constant.362.clone.1.flag_ref, f32[192,2816]{1,0:T(8,128)} %bitcast.10.refs_0_, f32[192,2816]{1,0:T(8,128)} %bitcast.11.refs_1_, f32[504,9192]{1,0:T(8,128)} %refs_1_.3), custom_call_target="tpu_custom_call" | custom-call | flops 1089994752 | bytes 10002432 | tf_op jit(solution)/shard_map/pallas_call | solution.py:86
  307.1 12.8 %shard_map.79.refs_3_ = f32[384,504]{1,0:T(8,128)} custom-call(s32[1]{0:T(128)} %constant.362.clone.1.flag_ref, f32[192,3072]{1,0:T(8,128)} %bitcast.8.refs_0_, f32[192,3072]{1,0:T(8,128)} %bitcast.9.refs_1_, f32[504,9192]{1,0:T(8,128)} %refs_1_.3, f32[384,504]{1,0:T(8,128)} %shard_map.78.refs_3_), custom_call_target="tpu_custom_call", output_to_operand_aliasing={{}: (4, {})} | custom-call | flops 1189085184 | bytes 10911744 | tf_op jit(solution)/shard_map/pallas_call | solution.py:86
  319.9 6.7 %shard_map.80.refs_3_ = f32[384,504]{1,0:T(8,128)} custom-call(s32[1]{0:T(128)} %constant.362.clone.1.flag_ref, f32[192,1280]{1,0:T(8,128)} %bitcast.6.refs_0_.refs_1_, f32[192,1280]{1,0:T(8,128)} %bitcast.7.refs_1_.refs_2_, f32[504,9192]{1,0:T(8,128)} %refs_1_.3, f32[384,504]{1,0:T(8,128)} %shard_map.79.refs_3_), custom_call_target="tpu_custom_call", output_to_operand_aliasing={{}: (4, {})} | custom-call | flops 495452160 | bytes 4546560 | tf_op jit(solution)/shard_map/pallas_call | solution.py:86
  326.6 4.5 shard_map.81.refs_3_
  331.1 4.5 shard_map.82
  354.5 10.1 %shard_map.83 = f32[192,504]{1,0:T(8,128)} custom-call(s32[1]{0:T(128)} %constant.362.clone.1.flag_ref, f32[192,2816]{1,0:T(8,128)} %bitcast.23.refs_0_, f32[504,9192]{1,0:T(8,128)} %refs_1_.3), custom_call_target="tpu_custom_call" | custom-call | flops 544997376 | bytes 7839744 | tf_op jit(solution)/shard_map/pallas_call | solution.py:86
  364.5 6.6 %shard_map.84.refs_4_ = f32[384,504]{1,0:T(8,128)} custom-call(s32[1]{0:T(128)} %bitcast.26.flag_ref, f32[192,1280]{1,0:T(8,128)} %get-tuple-element.18.refs_0_, f32[192,1280]{1,0:T(8,128)} %bitcast.6.refs_0_.refs_1_, f32[192,1280]{1,0:T(8,128)} %bitcast.7.refs_1_.refs_2_, f32[504,2304]{1,0:T(8,128)} %collective-permute-done.22.refs_3_), custom_call_target="tpu_custom_call" | custom-call | flops 495452160 | bytes 5529600 | tf_op jit(solution)/shard_map/pallas_call | solution.py:86
  371.2 5.9 %shard_map.85 = f32[384,504]{1,0:T(8,128)} custom-call(s32[1]{0:T(128)} %bitcast.26.flag_ref, f32[192,1024]{1,0:T(8,128)} %get-tuple-element.20.refs_0_, f32[192,1024]{1,0:T(8,128)} %bitcast.123, f32[192,1024]{1,0:T(8,128)} %bitcast.125, f32[504,2304]{1,0:T(8,128)} %collective-permute-done.22.refs_3_, ...), custom_call_target="tpu_custom_call", output_to_operand_aliasing={{}: (5, {})} | custom-call | flops 396361728 | bytes 4423680 | tf_op jit(solution)/shard_map/pallas_call | solution.py:86
  393.6 5.6 %fusion.2 = f32[192,504]{1,0:T(8,128)S(1)} fusion(f32[3072,192]{0,1:T(8,128)S(1)} %add.287, f32[504,9192]{1,0:T(8,128)} %refs_1_.3), kind=kOutput, calls=%fused_computation.2 | convolution fusion | flops 1783627776 | bytes 8939520 | tf_op jit(solution)/shard_map/dot_general | solution.py:106
  401.4 27.4 %collective-permute-done.19 = f32[2816,192]{0,1:T(8,128)} collective-permute-done((f32[2816,192]{0,1:T(8,128)}, f32[2816,192]{0,1:T(8,128)}, u32[]{:S(2)}, u32[]{:S(2)}) %collective-permute-start.19) | collective-permute-done | bytes 2162720 | tf_op jit(solution)/shard_map/ppermute | solution.py:162
  440.0 38.8 %collective-permute-done.25 = f32[3072,192]{0,1:T(8,128)S(1)} collective-permute-done((f32[3072,192]{0,1:T(8,128)S(1)}, f32[3072,192]{0,1:T(8,128)S(1)}, u32[]{:S(2)}, u32[]{:S(2)}) %collective-permute-start.25) | collective-permute-done | bytes 2359328 | tf_op jit(solution)/shard_map/ppermute | solution.py:162
  485.9 6.5 %collective-permute-done.14 = f32[3,24,504]{2,1,0:T(8,128)S(1)} collective-permute-done((f32[3,24,504]{2,1,0:T(8,128)S(1)}, f32[3,24,504]{2,1,0:T(8,128)S(1)}, u32[]{:S(2)}, u32[]{:S(2)}) %collective-permute-start.14) | collective-permute-done | bytes 145184 | tf_op jit(solution)/shard_map/ppermute | solution.py:240
  504.7 6.0 %collective-permute-start.35 = (f32[24,504]{1,0:T(8,128)S(1)}, f32[24,504]{1,0:T(8,128)S(1)}, u32[]{:S(2)}, u32[]{:S(2)}) collective-permute-start(f32[24,504]{1,0:T(8,128)S(1)} %get-tuple-element.36), channel_id=1, source_target_pairs={{0,24},{8,16},{20,12},{28,4},{1,25},{9,17},{21,13},{29,5},{2,26},{... | collective-permute-start | bytes 145160 | tf_op jit(solution)/shard_map/ppermute | solution.py:258
  512.7 4.7 collective-permute-done.39
  (180 shorter events, 111.6 us)
Async XLA Ops:
  9.3 121.6 %collective-permute-start.8 = (f32[2816,192]{0,1:T(8,128)S(1)}, f32[2816,192]{0,1:T(8,128)}, u32[]{:S(2)}, u32[]{:S(2)}) collective-permute-start(f32[2816,192]{0,1:T(8,128)S(1)} %slice.73), channel_id=1, source_target_pairs={{0,8},{8,16},{16,24},{1,9},{9,17},{17,25},{2,10},{10,18},{18,26},{... | collective-permute-start | bytes 6488072 | tf_op jit(solution)/shard_map/ppermute | solution.py:140
  16.9 71.0 %collective-permute-start.2 = (f32[1024,192]{0,1:T(8,128)S(1)}, f32[1024,192]{0,1:T(8,128)S(1)}, u32[]{:S(2)}, u32[]{:S(2)}) collective-permute-start(f32[1024,192]{0,1:T(8,128)S(1)} %get-tuple-element.19), channel_id=1, source_target_pairs={{0,8},{8,16},{1,9},{9,17},{2,10},{10,18},{3,11},{11,19},{4,12},{12... | collective-permute-start | bytes 2359304 | tf_op jit(solution)/shard_map/ppermute | solution.py:140
  22.5 85.4 %collective-permute-start.4 = (f32[1280,192]{0,1:T(8,128)S(1)}, f32[1280,192]{0,1:T(8,128)}, u32[]{:S(2)}, u32[]{:S(2)}) collective-permute-start(f32[1280,192]{0,1:T(8,128)S(1)} %get-tuple-element.17), channel_id=1, source_target_pairs={{0,8},{8,16},{1,9},{9,17},{2,10},{10,18},{3,11},{11,19},{4,12},{12... | collective-permute-start | bytes 2949128 | tf_op jit(solution)/shard_map/ppermute | solution.py:140
  25.3 63.3 %collective-permute-start.3 = (f32[1024,192]{0,1:T(8,128)S(1)}, f32[1024,192]{0,1:T(8,128)S(1)}, u32[]{:S(2)}, u32[]{:S(2)}) collective-permute-start(f32[1024,192]{0,1:T(8,128)S(1)} %get-tuple-element.19), channel_id=1, source_target_pairs={{24,16},{16,8},{25,17},{17,9},{26,18},{18,10},{27,19},{19,11},{28,... | collective-permute-start | bytes 2359304 | tf_op jit(solution)/shard_map/ppermute | solution.py:141
  26.3 87.1 %collective-permute-start.5 = (f32[1280,192]{0,1:T(8,128)S(1)}, f32[1280,192]{0,1:T(8,128)}, u32[]{:S(2)}, u32[]{:S(2)}) collective-permute-start(f32[1280,192]{0,1:T(8,128)S(1)} %get-tuple-element.17), channel_id=1, source_target_pairs={{24,16},{16,8},{25,17},{17,9},{26,18},{18,10},{27,19},{19,11},{28,... | collective-permute-start | bytes 2949128 | tf_op jit(solution)/shard_map/ppermute | solution.py:141
  87.9 36.0 %collective-permute-start.23 = (f32[1024,192]{0,1:T(8,128)S(1)}, f32[1024,192]{0,1:T(8,128)S(1)}, u32[]{:S(2)}, u32[]{:S(2)}) collective-permute-start(f32[1024,192]{0,1:T(8,128)S(1)} %collective-permute-done.2), channel_id=1, source_target_pairs={{8,16},{9,17},{10,18},{11,19},{12,20},{13,21},{14,22},{15,23}} | collective-permute-start | bytes 2359304 | tf_op jit(solution)/shard_map/ppermute | solution.py:140
  88.6 52.1 %collective-permute-start.9 = (f32[2816,192]{0,1:T(8,128)S(1)}, f32[2816,192]{0,1:T(8,128)}, u32[]{:S(2)}, u32[]{:S(2)}) collective-permute-start(f32[2816,192]{0,1:T(8,128)S(1)} %slice.73), channel_id=1, source_target_pairs={{24,16},{16,8},{8,0},{25,17},{17,9},{9,1},{26,18},{18,10},{10,2},{... | collective-permute-start | bytes 6488072 | tf_op jit(solution)/shard_map/ppermute | solution.py:141
  113.4 236.9 %collective-permute-start.22 = (f32[504,2304]{1,0:T(8,128)}, f32[504,2304]{1,0:T(8,128)}, u32[]{:S(2)}, u32[]{:S(2)}) collective-permute-start(f32[504,2304]{1,0:T(8,128)} %slice.80), channel_id=1, source_target_pairs={{0,8},{24,16},{1,9},{25,17},{2,10},{26,18},{3,11},{27,19},{4,12},{... | collective-permute-start | bytes 13934600 | tf_op jit(solution)/shard_map/ppermute | solution.py:150
  124.0 144.0 %collective-permute-start.6 = (f32[3072,192]{0,1:T(8,128)}, f32[3072,192]{0,1:T(8,128)}, u32[]{:S(2)}, u32[]{:S(2)}) collective-permute-start(f32[3072,192]{0,1:T(8,128)} %slice.72), channel_id=1, source_target_pairs={{0,8},{8,16},{16,24},{1,9},{9,17},{17,25},{2,10},{10,18},{18,26},{... | collective-permute-start | bytes 7077896 | tf_op jit(solution)/shard_map/ppermute | solution.py:140
  129.6 142.8 %collective-permute-start.7 = (f32[3072,192]{0,1:T(8,128)}, f32[3072,192]{0,1:T(8,128)}, u32[]{:S(2)}, u32[]{:S(2)}) collective-permute-start(f32[3072,192]{0,1:T(8,128)} %slice.72), channel_id=1, source_target_pairs={{24,16},{16,8},{8,0},{25,17},{17,9},{9,1},{26,18},{18,10},{10,2},{... | collective-permute-start | bytes 7077896 | tf_op jit(solution)/shard_map/ppermute | solution.py:141
  130.9 143.6 %collective-permute-start.15 = (f32[2816,192]{0,1:T(8,128)}, f32[2816,192]{0,1:T(8,128)}, u32[]{:S(2)}, u32[]{:S(2)}) collective-permute-start(f32[2816,192]{0,1:T(8,128)} %collective-permute-done.8), channel_id=1, source_target_pairs={{8,16},{16,24},{9,17},{17,25},{10,18},{18,26},{11,19},{19,27},{12,... | collective-permute-start | bytes 6488072 | tf_op jit(solution)/shard_map/ppermute | solution.py:140
  140.7 198.1 %collective-permute-start.16 = (f32[2816,192]{0,1:T(8,128)}, f32[2816,192]{0,1:T(8,128)}, u32[]{:S(2)}, u32[]{:S(2)}) collective-permute-start(f32[2816,192]{0,1:T(8,128)} %collective-permute-done.9), channel_id=1, source_target_pairs={{16,8},{8,0},{17,9},{9,1},{18,10},{10,2},{19,11},{11,3},{20,12},{1... | collective-permute-start | bytes 6488072 | tf_op jit(solution)/shard_map/ppermute | solution.py:141
  267.9 79.1 %collective-permute-start.28 = (f32[504,1000]{0,1:T(8,128)}, f32[504,1000]{0,1:T(8,128)S(1)}, u32[]{:S(2)}, u32[]{:S(2)}) collective-permute-start(f32[504,1000]{0,1:T(8,128)} %copy.24), channel_id=1, source_target_pairs={{0,8},{24,16},{1,9},{25,17},{2,10},{26,18},{3,11},{27,19},{4,12},{... | collective-permute-start | bytes 6048008 | tf_op jit(solution)/shard_map/ppermute | solution.py:150
  272.4 107.3 %collective-permute-start.17 = (f32[3072,192]{0,1:T(8,128)}, f32[3072,192]{0,1:T(8,128)}, u32[]{:S(2)}, u32[]{:S(2)}) collective-permute-start(f32[3072,192]{0,1:T(8,128)} %collective-permute-done.6), channel_id=1, source_target_pairs={{8,16},{16,24},{9,17},{17,25},{10,18},{18,26},{11,19},{19,27},{12,... | collective-permute-start | bytes 7077896 | tf_op jit(solution)/shard_map/ppermute | solution.py:140
  274.5 106.1 %collective-permute-start.18 = (f32[3072,192]{0,1:T(8,128)}, f32[3072,192]{0,1:T(8,128)}, u32[]{:S(2)}, u32[]{:S(2)}) collective-permute-start(f32[3072,192]{0,1:T(8,128)} %collective-permute-done.7), channel_id=1, source_target_pairs={{16,8},{8,0},{17,9},{9,1},{18,10},{10,2},{19,11},{11,3},{20,12},{1... | collective-permute-start | bytes 7077896 | tf_op jit(solution)/shard_map/ppermute | solution.py:141
  347.0 40.6 %collective-permute-start.20 = (f32[1280,192]{0,1:T(8,128)}, f32[1280,192]{0,1:T(8,128)}, u32[]{:S(2)}, u32[]{:S(2)}) collective-permute-start(f32[1280,192]{0,1:T(8,128)} %collective-permute-done.4), channel_id=1, source_target_pairs={{8,16},{9,17},{10,18},{11,19},{12,20},{13,21},{14,22},{15,23}} | collective-permute-start | bytes 2949128 | tf_op jit(solution)/shard_map/ppermute | solution.py:140
  348.6 39.7 %collective-permute-start.21 = (f32[1280,192]{0,1:T(8,128)}, f32[1280,192]{0,1:T(8,128)}, u32[]{:S(2)}, u32[]{:S(2)}) collective-permute-start(f32[1280,192]{0,1:T(8,128)} %collective-permute-done.5), channel_id=1, source_target_pairs={{16,8},{17,9},{18,10},{19,11},{20,12},{21,13},{22,14},{23,15}} | collective-permute-start | bytes 2949128 | tf_op jit(solution)/shard_map/ppermute | solution.py:141
  350.3 78.5 %collective-permute-start.19 = (f32[2816,192]{0,1:T(8,128)}, f32[2816,192]{0,1:T(8,128)}, u32[]{:S(2)}, u32[]{:S(2)}) collective-permute-start(f32[2816,192]{0,1:T(8,128)} %add.286), channel_id=1, source_target_pairs={{8,0},{16,24},{9,1},{17,25},{10,2},{18,26},{11,3},{19,27},{12,4},{... | collective-permute-start | bytes 6488072 | tf_op jit(solution)/shard_map/ppermute | solution.py:162
  379.7 57.8 %collective-permute-start.26 = (f32[1000,192]{0,1:T(8,128)S(1)}, f32[1000,192]{0,1:T(8,128)S(1)}, u32[]{:S(2)}, u32[]{:S(2)}) collective-permute-start(f32[1000,192]{0,1:T(8,128)S(1)} %copy-done.6), channel_id=1, source_target_pairs={{8,16},{9,17},{10,18},{11,19},{12,20},{13,21},{14,22},{15,23}} | collective-permute-start | bytes 2304008 | tf_op jit(solution)/shard_map/ppermute | solution.py:140
  383.4 95.4 %collective-permute-start.25 = (f32[3072,192]{0,1:T(8,128)S(1)}, f32[3072,192]{0,1:T(8,128)S(1)}, u32[]{:S(2)}, u32[]{:S(2)}) collective-permute-start(f32[3072,192]{0,1:T(8,128)S(1)} %add.287), channel_id=1, source_target_pairs={{8,0},{16,24},{9,1},{17,25},{10,2},{18,26},{11,3},{19,27},{12,4},{... | collective-permute-start | bytes 7077896 | tf_op jit(solution)/shard_map/ppermute | solution.py:162
  387.6 51.5 %collective-permute-start.27 = (f32[1000,192]{0,1:T(8,128)S(1)}, f32[1000,192]{0,1:T(8,128)S(1)}, u32[]{:S(2)}, u32[]{:S(2)}) collective-permute-start(f32[1000,192]{0,1:T(8,128)S(1)} %copy-done.4), channel_id=1, source_target_pairs={{16,8},{17,9},{18,10},{19,11},{20,12},{21,13},{22,14},{23,15}} | collective-permute-start | bytes 2304008 | tf_op jit(solution)/shard_map/ppermute | solution.py:141
  388.3 94.9 %collective-permute-start.11 = (f32[3,24,504]{2,1,0:T(8,128)S(1)}, f32[3,24,504]{2,1,0:T(8,128)S(1)}, u32[]{:S(2)}, u32[]{:S(2)}) collective-permute-start(f32[3,24,504]{2,1,0:T(8,128)S(1)} %copy-done.18), channel_id=1, source_target_pairs={{0,4},{1,5},{2,6},{3,7},{4,0},{5,1},{6,2},{7,3},{8,12},{9,13},{10,... | collective-permute-start | bytes 435464 | tf_op jit(solution)/shard_map/ppermute | solution.py:231
  428.8 54.5 %collective-permute-start.12 = (f32[3,24,504]{2,1,0:T(8,128)S(1)}, f32[3,24,504]{2,1,0:T(8,128)S(1)}, u32[]{:S(2)}, u32[]{:S(2)}) collective-permute-start(f32[3,24,504]{2,1,0:T(8,128)S(1)} %copy-done.17), channel_id=1, source_target_pairs={{0,2},{1,3},{2,0},{3,1},{4,6},{5,7},{6,4},{7,5},{8,10},{9,11},{10,... | collective-permute-start | bytes 435464 | tf_op jit(solution)/shard_map/ppermute | solution.py:231
  437.5 45.8 %collective-permute-start.13 = (f32[3,24,504]{2,1,0:T(8,128)S(1)}, f32[3,24,504]{2,1,0:T(8,128)S(1)}, u32[]{:S(2)}, u32[]{:S(2)}) collective-permute-start(f32[3,24,504]{2,1,0:T(8,128)S(1)} %get-tuple-element.27), channel_id=1, source_target_pairs={{0,6},{1,7},{2,4},{3,5},{4,2},{5,3},{6,0},{7,1},{8,14},{9,15},{10,... | collective-permute-start | bytes 435464 | tf_op jit(solution)/shard_map/ppermute | solution.py:231
  (45 other events, 711.9 us)
